TPU v7x, 128 devices: a whole 4x4x4 slice. The times are simulated.
128 devices in a mesh: lat: 4 (over z), lon: 32 (over x, y, core).
Axes of the slice: x: 4, y: 4, z: 4, core: 2. Of those that a mesh axis runs over, the one named last changes fastest.
Arguments:
- spectrum: float32 [1296, 32, 8192], P(None, 'lat', 'lon'), may hold values from 0.01 to 1
- sea_mask: int32 [32, 8192], P('lat', 'lon'), may hold values 0 or 1
- courant: float32 [2, 1296], replicated, may hold values from -0.45 to 0.45
- obs_tile: int32 [32768, 1], P(('lat', 'lon')), may hold values from 0 to 127; in each aligned block of 256 rows (0 to 255, 256 to 511, ...) at most 8 rows name the same one
- obs_cell: int32 [32768], P(('lat', 'lon')), may hold values from 0 to 2047
- obs_value: float32 [32768], P(('lat', 'lon')), may hold values from 1 to 3
- obs_error: float32 [32768], P(('lat', 'lon')), may hold values from 0.05 to 0.5
Outputs:
- updated: float32 [1296, 32, 8192], P(None, 'lat', 'lon')
- increment: float32 [32, 8192], P('lat', 'lon')
Inputs may be any that keep to these rules, and one draw needn't show every extreme that they name: `obs_tile`: within the 256 reports of one device no tile occurs more than 8 times.
All inputs are finite; a program needn't handle non-finite values. No bound on the sum of `sea_mask` on one device may be relied on, other than what follows from the above.
Results may differ from a plain program's by a relative error of at most 0.00002.
Values sent between devices are 32-bit elements; how exact they have to be, the bound alone decides.
A program may use at most 128 MiB of HBM per device.

v0:
```python
import jax
import jax.numpy as jnp
from jax import lax
from jax.sharding import PartitionSpec as P

PASSES = 8
spread_rate = 0.2
prior_weight = 4.0


def with_halo(array, sides, width):
    edges = {}
    for axis, dim in sides:
        size, length = (lax.axis_size(axis), array.shape[dim])
        up = [(i, (i + 1) % size) for i in range(size)]
        last = lax.slice_in_dim(array, length - width, length, axis=dim)
        leading = lax.slice_in_dim(array, 0, width, axis=dim)
        edges[dim] = (
            lax.ppermute(last, axis, up),
            lax.ppermute(leading, axis, [(b, a) for a, b in up]),
        )
    done = []
    for _, dim in sides:
        low, high = edges[dim]
        around = [(width, width) if d in done else (0, 0) for d in range(array.ndim)]
        array = jnp.concatenate([jnp.pad(low, around), array, jnp.pad(high, around)], axis=dim)
        done.append(dim)
    return array


def with_halo_2(cells, sides, width):
    for axis, dim in sides:
        count = lax.axis_size(axis)
        head = lax.slice_in_dim(cells, 0, width, axis=dim)
        tail = lax.slice_in_dim(cells, cells.shape[dim] - width, cells.shape[dim], axis=dim)
        cells = jnp.concatenate(
            [
                lax.ppermute(tail, axis, [(i, (i + 1) % count) for i in range(count)]),
                cells,
                lax.ppermute(head, axis, [((i + 1) % count, i) for i in range(count)]),
            ],
            axis=dim,
        )
    return cells


def relax_pass(fields, sea_ext):
    centre = fields[:, 1:-1, 1:-1]
    summed = sea_ext[2:, 1:-1] * (fields[:, 2:, 1:-1] - centre)
    summed = summed + sea_ext[:-2, 1:-1] * (fields[:, :-2, 1:-1] - centre)
    summed = summed + sea_ext[1:-1, 2:] * (fields[:, 1:-1, 2:] - centre)
    summed = summed + sea_ext[1:-1, :-2] * (fields[:, 1:-1, :-2] - centre)
    return centre + spread_rate * sea_ext[1:-1, 1:-1] * summed


def body(spectrum, sea_mask, courant, obs_tile, obs_cell, obs_value, obs_error):
    tile_rows, tile_cols = sea_mask.shape
    lat_count = lax.axis_size("lat")
    lon_count = lax.axis_size("lon")
    devices = lat_count * lon_count
    report_count = obs_value.shape[0]
    slot_cap = max(8, 4 * report_count // devices)
    outer_rim = with_halo(spectrum, (("lat", 1), ("lon", 2)), 1)
    height = 4.0 * jnp.sqrt(jnp.mean(spectrum, axis=0))
    height_flat = height.reshape(-1)
    weights = 1.0 / obs_error
    owners = obs_tile[:, 0]
    blank_grid = jnp.zeros((2, tile_rows * tile_cols), jnp.float32)
    position = jnp.arange(report_count, dtype=jnp.int32)
    earlier = (owners[:, None] == owners[None, :]) & (position[None, :] < position[:, None])
    slot_index = jnp.sum(earlier.astype(jnp.int32), axis=1)
    reports = jnp.stack([obs_value, weights, obs_cell.astype(jnp.float32)])
    outbox = (
        jnp.zeros((3, devices, slot_cap), jnp.float32)
        .at[:, owners, slot_index]
        .set(reports)
        .reshape(3, lat_count, lon_count, slot_cap)
    )
    arrived = lax.all_to_all(
        lax.all_to_all(outbox, "lat", split_axis=1, concat_axis=1, tiled=True),
        "lon",
        split_axis=2,
        concat_axis=2,
        tiled=True,
    ).reshape(3, -1)
    totals = blank_grid
    cell_ids = arrived[2].astype(jnp.int32)
    report_weights = arrived[1]
    misfit = report_weights * (arrived[0] - height_flat[cell_ids])
    totals = totals.at[0, cell_ids].add(misfit)
    totals = totals.at[1, cell_ids].add(report_weights)
    ocean = sea_mask.astype(jnp.float32)
    fields = totals.reshape(2, tile_rows, tile_cols) * ocean
    halo_depth = 2
    coast_ext = with_halo_2(sea_mask, (("lat", 0), ("lon", 1)), halo_depth)
    lat_line = (
        lax.axis_index("lat") * tile_rows
        + jnp.arange(tile_rows + 2 * halo_depth, dtype=jnp.int32)
        - halo_depth
    )
    inside = (lat_line >= 0) & (lat_line < lat_count * tile_rows)
    coast_ext = jnp.where(inside[:, None], coast_ext, 0).astype(jnp.float32)
    edge_sea = coast_ext[
        halo_depth - 1 : coast_ext.shape[0] - halo_depth + 1,
        halo_depth - 1 : coast_ext.shape[1] - halo_depth + 1,
    ]
    for repeat in range(PASSES // 2):
        padded = with_halo_2(fields, (("lat", 1), ("lon", 2)), 2)
        fields = relax_pass(relax_pass(padded, coast_ext), edge_sea)
    increment = ocean * fields[0] / (prior_weight + fields[1])
    factor = jnp.exp(2.0 * increment / height)
    rim_scale = with_halo_2(factor, (("lat", 0), ("lon", 1)), 1)
    analyzed = outer_rim * rim_scale
    east_speed = courant[0][:, None, None]
    north_speed = courant[1][:, None, None]
    row_band = analyzed[:, 1:-1, :]
    ocean_band = edge_sea[1:-1, :]
    flux_east = (
        (
            jnp.maximum(east_speed, 0.0) * row_band[:, :, :-1]
            + jnp.minimum(east_speed, 0.0) * row_band[:, :, 1:]
        )
        * ocean_band[:, :-1]
        * ocean_band[:, 1:]
    )
    col_strip = analyzed[:, :, 1:-1]
    ocean_strip = edge_sea[:, 1:-1]
    flux_north = (
        (
            jnp.maximum(north_speed, 0.0) * col_strip[:, :-1]
            + jnp.minimum(north_speed, 0.0) * col_strip[:, 1:]
        )
        * ocean_strip[:-1]
        * ocean_strip[1:]
    )
    centre = analyzed[:, 1:-1, 1:-1]
    updated = ocean * (
        centre
        - (flux_east[:, :, 1:] - flux_east[:, :, :-1])
        - (flux_north[:, 1:] - flux_north[:, :-1])
    )
    return (updated, increment)


def solution(mesh):
    return jax.shard_map(
        body,
        mesh=mesh,
        in_specs=(
            P(None, "lat", "lon"),
            P("lat", "lon"),
            P(),
            P(("lat", "lon"), None),
            P(("lat", "lon")),
            P(("lat", "lon")),
            P(("lat", "lon")),
        ),
        out_specs=(P(None, "lat", "lon"), P("lat", "lon")),
        check_vma=False,
    )
```

profile of v0, /device:TPU:1, one launch (start us, length us, event | category | flops | bytes accessed | tf_op | source)
XLA Modules:
  0.0 246.1 jit_solution(15258800450788764085)
XLA Ops:
  0.7 0.8 fusion.118
  1.5 2.5 collective-permute-start.8
  3.9 2.1 collective-permute-start.9
  7.4 0.9 convert_reduce_fusion
  9.9 11.5 %scatter_fusion = f32[3,128,8]{0,2,1:T(8,128)S(1)} fusion(f32[3,128,8]{0,2,1:T(8,128)S(1)} %broadcast_in_dim.13, s32[256]{0:T(256)S(1)} %bitcast.35, f32[256,3]{1,0:T(8,128)S(1)} %copy.52), kind=kCustom, calls=%fused_computation.1 | custom fusion | bytes 11264 | tf_op jit(solution)/shard_map/scatter | solution.py:76
  21.7 0.7 reshape.164
  22.4 3.3 %all-to-all-start = ((f32[4,1,768]{2,1,0:T(1,128)}), f32[4,1,768]{2,1,0:T(1,128)S(1)}, u32[]{:S(2)}, u32[]{:S(2)}) async-start(f32[4,1,768]{2,1,0:T(1,128)} %reshape.164), calls=%async_computation | async-start | bytes 24576 | tf_op jit(solution)/shard_map/all_to_all | solution.py:80
  25.6 4.8 %reduce_sum.22 = f32[8,256]{1,0:T(8,128)S(1)} reduce(f32[1296,8,256]{2,1,0:T(8,128)} %param.7, f32[]{:T(128)} %constant.15.clone.1), dimensions={0}, to_apply=%region_2.3 | reduce | flops 2652160 | bytes 10625028 | tf_op jit(solution)/shard_map/reduce_sum | solution.py:64
  30.6 2.2 collective-permute-start.10
  34.1 0.8 copy.54
  34.9 7.7 %all-to-all-start.1 = ((f32[3,4,32,8]{3,1,0,2:T(4,128)}), f32[3,4,32,8]{3,1,0,2:T(4,128)S(1)}, u32[]{:S(2)}, u32[]{:S(2)}) async-start(f32[3,4,32,8]{3,1,0,2:T(4,128)} %copy.54), calls=%async_computation.1 | async-start | bytes 393216 | tf_op jit(solution)/shard_map/all_to_all | solution.py:79
  42.6 8.2 %all-to-all-done.1 = f32[3,4,32,8]{3,1,0,2:T(4,128)S(1)} async-done(((f32[3,4,32,8]{3,1,0,2:T(4,128)}), f32[3,4,32,8]{3,1,0,2:T(4,128)S(1)}, u32[]{:S(2)}, u32[]{:S(2)}) %all-to-all-start.1) | async-done | bytes 12320 | tf_op jit(solution)/shard_map/all_to_all | solution.py:79
  51.6 6.2 %gather_fusion = f32[1024]{0:T(1024)S(1)} fusion(f32[2048]{0:T(1024)S(1)} %bitcast.34, s32[1024]{0:T(1024)S(1)} %broadcast_clamp_fusion), kind=kCustom, calls=%fused_computation | custom fusion | bytes 12288 | tf_op jit(solution)/shard_map/gather | solution.py:89
  57.8 7.0 %scatter_custom_fusion.1 = f32[4096]{0:T(1024)S(1)} fusion(s32[1024]{0:T(1024)S(1)} %get-tuple-element.64, f32[1024]{0:T(1024)S(1)} %subtract_multiply_fusion, f32[]{:T(128)} %constant.15.clone.1), kind=kCustom, calls=%fused_computation.182 | custom fusion | flops 1024 | bytes 16388
  64.8 7.1 %scatter_fusion.1 = f32[4096]{0:T(1024)S(1)} fusion(f32[4096]{0:T(1024)S(1)} %scatter_custom_fusion.1, s32[1024]{0:T(1024)S(1)} %get-tuple-element.63, f32[1024]{0:T(1024)S(1)} %reshape.154), kind=kCustom, calls=%fused_computation.3 | custom fusion | flops 1024 | bytes 16384
  71.9 2.1 collective-permute-start.4
  74.7 0.9 collective-permute-done.4
  75.6 1.0 collective-permute-done.5
  76.7 1.5 collective-permute-start.7
  78.5 1.3 collective-permute-done.7
  80.3 0.8 collective-permute-start.12
  81.1 1.9 collective-permute-start.13
  83.0 9.2 %fusion.102 = (f32[1296,1,256]{2,1,0:T(1,128)S(1)}, f32[1296,1,256]{2,1,0:T(1,128)S(1)}) fusion(f32[1296,8,256]{2,1,0:T(8,128)} %param.7), kind=kLoop, calls=%fused_computation.205 | loop fusion | bytes 5308416 | tf_op jit(solution)/shard_map/slice | solution.py:16
  92.3 1.0 collective-permute-start.2
  93.4 5.8 %collective-permute-start.15 = (f32[2,12,2]{2,1,0:T(8,128)S(1)}, f32[2,12,2]{2,1,0:T(8,128)S(1)}, u32[]{:S(2)}, u32[]{:S(2)}) collective-permute-start(f32[2,12,2]{2,1,0:T(8,128)S(1)} %get-tuple-element.29), channel_id=1, source_target_pairs={{1,0},{2,1},{3,2},{4,3},{5,4},{6,5},{7,6},{8,7},{9,8},{10,9},{11,1... | collective-permute-start | bytes 584 | tf_op jit(solution)/shard_map/ppermute | solution.py:40
  101.2 2.3 collective-permute-start.17
  103.5 7.5 %fusion.103 = (f32[1296,8,1]{2,1,0:T(8,128)}, f32[1296,8,1]{2,1,0:T(8,128)}) fusion(f32[1296,8,256]{2,1,0:T(8,128)} %param.7), kind=kLoop, calls=%fused_computation.206 | loop fusion | bytes 165888 | tf_op jit(solution)/shard_map/slice | solution.py:16
  111.0 20.1 %collective-permute-done.16 = f32[2,2,256]{2,1,0:T(2,128)S(1)} collective-permute-done((f32[2,2,256]{2,1,0:T(2,128)S(1)}, f32[2,2,256]{2,1,0:T(2,128)S(1)}, u32[]{:S(2)}, u32[]{:S(2)}) %collective-permute-start.16) | collective-permute-done | bytes 4128 | tf_op jit(solution)/shard_map/ppermute | solution.py:38
  131.3 1.3 collective-permute-start.19
  133.0 4.1 %copy.63 = f32[1296,8,1]{0,1,2:T(8,128)S(1)} copy(f32[1296,8,1]{2,1,0:T(8,128)} %get-tuple-element.21) | data formatting | bytes 82944
  137.7 2.7 %collective-permute-start.21 = (f32[2,2,256]{2,1,0:T(2,128)S(1)}, f32[2,2,256]{2,1,0:T(2,128)S(1)}, u32[]{:S(2)}, u32[]{:S(2)}) collective-permute-start(f32[2,2,256]{2,1,0:T(2,128)S(1)} %get-tuple-element.50), channel_id=1, source_target_pairs={{32,0},{64,32},{96,64},{0,96},{33,1},{65,33},{97,65},{1,97},{34,2}... | collective-permute-start | bytes 12296 | tf_op jit(solution)/shard_map/ppermute | solution.py:40
  140.5 12.4 %copy.47 = f32[1296,8,256]{0,2,1:T(8,128)} copy(f32[1296,8,256]{2,1,0:T(8,128)} %param.7) | data formatting | bytes 21233664 | tf_op args[0]
  152.9 4.1 %copy.60 = f32[1296,8,1]{0,1,2:T(8,128)S(1)} copy(f32[1296,8,1]{2,1,0:T(8,128)} %get-tuple-element.20) | data formatting | bytes 82944
  157.1 5.2 %collective-permute-start.23 = (f32[2,12,2]{2,1,0:T(8,128)S(1)}, f32[2,12,2]{2,1,0:T(8,128)S(1)}, u32[]{:S(2)}, u32[]{:S(2)}) collective-permute-start(f32[2,12,2]{2,1,0:T(8,128)S(1)} %get-tuple-element.25), channel_id=1, source_target_pairs={{1,0},{2,1},{3,2},{4,3},{5,4},{6,5},{7,6},{8,7},{9,8},{10,9},{11,1... | collective-permute-start | bytes 584 | tf_op jit(solution)/shard_map/ppermute | solution.py:40
  162.4 0.8 collective-permute-done.23
  164.4 2.7 %collective-permute-start.25 = (f32[1,256]{1,0:T(1,128)S(1)}, f32[1,256]{1,0:T(1,128)S(1)}, u32[]{:S(2)}, u32[]{:S(2)}) collective-permute-start(f32[1,256]{1,0:T(1,128)S(1)} %get-tuple-element.60), channel_id=1, source_target_pairs={{32,0},{64,32},{96,64},{0,96},{33,1},{65,33},{97,65},{1,97},{34,2}... | collective-permute-start | bytes 3080 | tf_op jit(solution)/shard_map/ppermute | solution.py:40
  167.2 1.2 collective-permute-done.24
  168.4 2.8 %collective-permute-start = (f32[1296,8,1]{0,1,2:T(8,128)S(1)}, f32[1296,8,1]{0,1,2:T(8,128)S(1)}, u32[]{:S(2)}, u32[]{:S(2)}) collective-permute-start(f32[1296,8,1]{0,1,2:T(8,128)S(1)} %copy.60), channel_id=1, source_target_pairs={{0,1},{1,2},{2,3},{3,4},{4,5},{5,6},{6,7},{7,8},{8,9},{9,10},{10,1... | collective-permute-start | bytes 124424 | tf_op jit(solution)/shard_map/ppermute | solution.py:19
  171.3 4.1 %collective-permute-done.26 = f32[10,1]{1,0:T(8,128)S(1)} collective-permute-done((f32[10,1]{1,0:T(8,128)S(1)}, f32[10,1]{1,0:T(8,128)S(1)}, u32[]{:S(2)}, u32[]{:S(2)}) %collective-permute-start.26) | collective-permute-done | bytes 72 | tf_op jit(solution)/shard_map/ppermute | solution.py:38
  175.4 6.1 %collective-permute-start.27 = (f32[10,1]{1,0:T(8,128)S(1)}, f32[10,1]{1,0:T(8,128)S(1)}, u32[]{:S(2)}, u32[]{:S(2)}) collective-permute-start(f32[10,1]{1,0:T(8,128)S(1)} %get-tuple-element.48), channel_id=1, source_target_pairs={{1,0},{2,1},{3,2},{4,3},{5,4},{6,5},{7,6},{8,7},{9,8},{10,9},{11,1... | collective-permute-start | bytes 128 | tf_op jit(solution)/shard_map/ppermute | solution.py:40
  181.5 0.8 collective-permute-done.27
  182.5 1.8 copy.48
  184.3 1.8 copy.46
  186.1 14.5 %fusion = f32[1296,10,258]{0,2,1:T(8,128)S(1)} fusion(f32[1296,8,1]{0,2,1:T(1,128)S(1)} %copy.66, f32[1296,8,1]{0,2,1:T(1,128)S(1)} %copy.65, f32[1296,1,256]{0,2,1:T(8,128)S(1)} %copy.48, f32[1296,8,256]{0,2,1:T(8,128)} %copy.47, f32[1296,1,256]{0,2,1:T(8,128)S(1)} %copy.46, f32[10,258]{1,0:T(8,128)S(1)} %pad_maximum_fusion.32), kind=kLoop, calls=%fused_computation.5 | loop fusion | flops 30093120 | bytes 26739024 | tf_op jit(solution)/shard_map/mul | solution.py:113
  200.5 5.9 %fusion.6 = f32[1296,8,257]{0,2,1:T(8,128)} fusion(f32[1296,10,258]{0,2,1:T(8,128)S(1)} %fusion, f32[8,257]{1,0:T(8,128)S(1)} %get-tuple-element.34, f32[8,257]{1,0:T(8,128)S(1)} %get-tuple-element.33, f32[1296]{0:T(1024)S(1)} %get-tuple-element.9, f32[1296]{0:T(1024)S(1)} %get-tuple-element.8), kind=kLoop, calls=%fused_computation.17 | loop fusion | flops 13322880 | bytes 32001728 | tf_op jit(solution)/shard_map/mul | solution.py:119
  206.4 7.3 %fusion.3 = f32[1296,9,256]{0,2,1:T(8,128)} fusion(f32[1296,10,258]{0,2,1:T(8,128)S(1)} %fusion, f32[9,256]{1,0:T(8,128)S(1)} %get-tuple-element.36, f32[9,256]{1,0:T(8,128)S(1)} %get-tuple-element.35, f32[1296]{0:T(1024)S(1)} %get-tuple-element.10, f32[1296]{0:T(1024)S(1)} %get-tuple-element.11), kind=kLoop, calls=%fused_computation.12 | loop fusion | flops 14929920 | bytes 35860608 | tf_op jit(solution)/shard_map/mul | solution.py:129
  213.8 20.2 %fusion.8 = f32[1296,8,256]{0,2,1:T(8,128)} fusion(f32[1296,9,256]{0,2,1:T(8,128)} %fusion.3, f32[1296,8,257]{0,2,1:T(8,128)} %fusion.6, f32[1296,10,258]{0,2,1:T(8,128)S(1)} %fusion, f32[8,256]{1,0:T(8,128)S(1)} %convert_element_type.28), kind=kLoop, calls=%fused_computation.21 | loop fusion | flops 13271040 | bytes 63709184 | tf_op jit(solution)/shard_map/mul | solution.py:137
  234.0 12.1 %copy.59 = f32[1296,8,256]{2,1,0:T(8,128)} copy(f32[1296,8,256]{0,2,1:T(8,128)} %fusion.8) | data formatting | bytes 21233664
  (113 shorter events, 12.0 us)
Async XLA Ops:
  0.6 50.6 %copy-start.3 = (s32[2]{0:T(128)S(1)}, s32[2]{0:T(128)}, u32[]{:S(2)}) copy-start(s32[2]{0:T(128)} %constant.55) | copy-start | bytes 28
  0.6 50.7 %copy-start.2 = (s32[2]{0:T(128)S(1)}, s32[2]{0:T(128)}, u32[]{:S(2)}) copy-start(s32[2]{0:T(128)} %constant.52) | copy-start | bytes 28
  0.7 29.8 %copy-start = (s32[8,256]{1,0:T(8,128)S(1)}, s32[8,256]{1,0:T(8,128)}, u32[]{:S(2)}) copy-start(s32[8,256]{1,0:T(8,128)} %param.8) | copy-start | bytes 24580
  1.5 29.0 %collective-permute-start.8 = (s32[2,256]{1,0:T(2,128)S(1)}, s32[2,256]{1,0:T(2,128)S(1)}, u32[]{:S(2)}, u32[]{:S(2)}) collective-permute-start(s32[2,256]{1,0:T(2,128)S(1)} %get-tuple-element.61), channel_id=1, source_target_pairs={{0,32},{32,64},{64,96},{96,0},{1,33},{33,65},{65,97},{97,1},{2,34}... | collective-permute-start | bytes 6152 | tf_op jit(solution)/shard_map/ppermute | solution.py:38
  3.9 26.6 %collective-permute-start.9 = (s32[2,256]{1,0:T(2,128)S(1)}, s32[2,256]{1,0:T(2,128)S(1)}, u32[]{:S(2)}, u32[]{:S(2)}) collective-permute-start(s32[2,256]{1,0:T(2,128)S(1)} %get-tuple-element.62), channel_id=1, source_target_pairs={{32,0},{64,32},{96,64},{0,96},{33,1},{65,33},{97,65},{1,97},{34,2}... | collective-permute-start | bytes 6152 | tf_op jit(solution)/shard_map/ppermute | solution.py:40
  22.4 10.4 %all-to-all-start = ((f32[4,1,768]{2,1,0:T(1,128)}), f32[4,1,768]{2,1,0:T(1,128)S(1)}, u32[]{:S(2)}, u32[]{:S(2)}) async-start(f32[4,1,768]{2,1,0:T(1,128)} %reshape.164), calls=%async_computation | async-start | bytes 24576 | tf_op jit(solution)/shard_map/all_to_all | solution.py:80
  30.6 11.9 %collective-permute-start.10 = (s32[12,2]{1,0:T(8,128)S(1)}, s32[12,2]{1,0:T(8,128)S(1)}, u32[]{:S(2)}, u32[]{:S(2)}) collective-permute-start(s32[12,2]{1,0:T(8,128)S(1)} %get-tuple-element.55), channel_id=1, source_target_pairs={{0,1},{1,2},{2,3},{3,4},{4,5},{5,6},{6,7},{7,8},{8,9},{9,10},{10,1... | collective-permute-start | bytes 296 | tf_op jit(solution)/shard_map/ppermute | solution.py:38
  32.8 9.8 %collective-permute-start.11 = (s32[12,2]{1,0:T(8,128)S(1)}, s32[12,2]{1,0:T(8,128)S(1)}, u32[]{:S(2)}, u32[]{:S(2)}) collective-permute-start(s32[12,2]{1,0:T(8,128)S(1)} %get-tuple-element.56), channel_id=1, source_target_pairs={{1,0},{2,1},{3,2},{4,3},{5,4},{6,5},{7,6},{8,7},{9,8},{10,9},{11,1... | collective-permute-start | bytes 296 | tf_op jit(solution)/shard_map/ppermute | solution.py:40
  34.9 16.0 %all-to-all-start.1 = ((f32[3,4,32,8]{3,1,0,2:T(4,128)}), f32[3,4,32,8]{3,1,0,2:T(4,128)S(1)}, u32[]{:S(2)}, u32[]{:S(2)}) async-start(f32[3,4,32,8]{3,1,0,2:T(4,128)} %copy.54), calls=%async_computation.1 | async-start | bytes 393216 | tf_op jit(solution)/shard_map/all_to_all | solution.py:79
  71.9 3.7 %collective-permute-start.4 = (f32[2,2,256]{2,1,0:T(2,128)S(1)}, f32[2,2,256]{2,1,0:T(2,128)S(1)}, u32[]{:S(2)}, u32[]{:S(2)}) collective-permute-start(f32[2,2,256]{2,1,0:T(2,128)S(1)} %get-tuple-element.57), channel_id=1, source_target_pairs={{0,32},{32,64},{64,96},{96,0},{1,33},{33,65},{65,97},{97,1},{2,34}... | collective-permute-start | bytes 12296 | tf_op jit(solution)/shard_map/ppermute | solution.py:38
  74.0 2.6 %collective-permute-start.5 = (f32[2,2,256]{2,1,0:T(2,128)S(1)}, f32[2,2,256]{2,1,0:T(2,128)S(1)}, u32[]{:S(2)}, u32[]{:S(2)}) collective-permute-start(f32[2,2,256]{2,1,0:T(2,128)S(1)} %get-tuple-element.58), channel_id=1, source_target_pairs={{32,0},{64,32},{96,64},{0,96},{33,1},{65,33},{97,65},{1,97},{34,2}... | collective-permute-start | bytes 12296 | tf_op jit(solution)/shard_map/ppermute | solution.py:40
  76.7 3.2 %collective-permute-start.7 = (f32[2,12,2]{2,1,0:T(8,128)S(1)}, f32[2,12,2]{2,1,0:T(8,128)S(1)}, u32[]{:S(2)}, u32[]{:S(2)}) collective-permute-start(f32[2,12,2]{2,1,0:T(8,128)S(1)} %get-tuple-element.31), channel_id=1, source_target_pairs={{1,0},{2,1},{3,2},{4,3},{5,4},{6,5},{7,6},{8,7},{9,8},{10,9},{11,1... | collective-permute-start | bytes 584 | tf_op jit(solution)/shard_map/ppermute | solution.py:40
  78.2 1.7 collective-permute-start.6
  80.3 13.1 %collective-permute-start.12 = (f32[2,2,256]{2,1,0:T(2,128)S(1)}, f32[2,2,256]{2,1,0:T(2,128)S(1)}, u32[]{:S(2)}, u32[]{:S(2)}) collective-permute-start(f32[2,2,256]{2,1,0:T(2,128)S(1)} %get-tuple-element.53), channel_id=1, source_target_pairs={{0,32},{32,64},{64,96},{96,0},{1,33},{33,65},{65,97},{97,1},{2,34}... | collective-permute-start | bytes 12296 | tf_op jit(solution)/shard_map/ppermute | solution.py:38
  81.1 12.2 %collective-permute-start.13 = (f32[2,2,256]{2,1,0:T(2,128)S(1)}, f32[2,2,256]{2,1,0:T(2,128)S(1)}, u32[]{:S(2)}, u32[]{:S(2)}) collective-permute-start(f32[2,2,256]{2,1,0:T(2,128)S(1)} %get-tuple-element.54), channel_id=1, source_target_pairs={{32,0},{64,32},{96,64},{0,96},{33,1},{65,33},{97,65},{1,97},{34,2}... | collective-permute-start | bytes 12296 | tf_op jit(solution)/shard_map/ppermute | solution.py:40
  92.3 90.2 %collective-permute-start.2 = (f32[1296,1,256]{2,0,1:T(8,128)S(1)}, f32[1296,1,256]{2,0,1:T(8,128)}, u32[]{:S(2)}, u32[]{:S(2)}) collective-permute-start(f32[1296,1,256]{2,0,1:T(8,128)S(1)} %copy.62), channel_id=1, source_target_pairs={{32,0},{64,32},{96,64},{0,96},{33,1},{65,33},{97,65},{1,97},{34,2}... | collective-permute-start | bytes 3981320 | tf_op jit(solution)/shard_map/ppermute | solution.py:20
  93.4 6.7 %collective-permute-start.15 = (f32[2,12,2]{2,1,0:T(8,128)S(1)}, f32[2,12,2]{2,1,0:T(8,128)S(1)}, u32[]{:S(2)}, u32[]{:S(2)}) collective-permute-start(f32[2,12,2]{2,1,0:T(8,128)S(1)} %get-tuple-element.29), channel_id=1, source_target_pairs={{1,0},{2,1},{3,2},{4,3},{5,4},{6,5},{7,6},{8,7},{9,8},{10,9},{11,1... | collective-permute-start | bytes 584 | tf_op jit(solution)/shard_map/ppermute | solution.py:40
  99.2 1.2 collective-permute-start.14
  99.3 85.0 %collective-permute-start.1 = (f32[1296,1,256]{2,0,1:T(8,128)S(1)}, f32[1296,1,256]{2,0,1:T(8,128)}, u32[]{:S(2)}, u32[]{:S(2)}) collective-permute-start(f32[1296,1,256]{2,0,1:T(8,128)S(1)} %copy.61), channel_id=1, source_target_pairs={{0,32},{32,64},{64,96},{96,0},{1,33},{33,65},{65,97},{97,1},{2,34}... | collective-permute-start | bytes 3981320 | tf_op jit(solution)/shard_map/ppermute | solution.py:19
  100.8 30.4 %collective-permute-start.16 = (f32[2,2,256]{2,1,0:T(2,128)S(1)}, f32[2,2,256]{2,1,0:T(2,128)S(1)}, u32[]{:S(2)}, u32[]{:S(2)}) collective-permute-start(f32[2,2,256]{2,1,0:T(2,128)S(1)} %get-tuple-element.51), channel_id=1, source_target_pairs={{0,32},{32,64},{64,96},{96,0},{1,33},{33,65},{65,97},{97,1},{2,34}... | collective-permute-start | bytes 12296 | tf_op jit(solution)/shard_map/ppermute | solution.py:38
  101.2 39.2 %copy-start.1 = (f32[2,1296]{1,0:T(2,128)S(1)}, f32[2,1296]{1,0:T(2,128)}, u32[]{:S(2)}) copy-start(f32[2,1296]{1,0:T(2,128)} %param.9) | copy-start | bytes 31108
  101.2 29.9 %collective-permute-start.17 = (f32[2,2,256]{2,1,0:T(2,128)S(1)}, f32[2,2,256]{2,1,0:T(2,128)S(1)}, u32[]{:S(2)}, u32[]{:S(2)}) collective-permute-start(f32[2,2,256]{2,1,0:T(2,128)S(1)} %get-tuple-element.52), channel_id=1, source_target_pairs={{32,0},{64,32},{96,64},{0,96},{33,1},{65,33},{97,65},{1,97},{34,2}... | collective-permute-start | bytes 12296 | tf_op jit(solution)/shard_map/ppermute | solution.py:40
  131.3 6.0 %collective-permute-start.19 = (f32[2,12,2]{2,1,0:T(8,128)S(1)}, f32[2,12,2]{2,1,0:T(8,128)S(1)}, u32[]{:S(2)}, u32[]{:S(2)}) collective-permute-start(f32[2,12,2]{2,1,0:T(8,128)S(1)} %get-tuple-element.27), channel_id=1, source_target_pairs={{1,0},{2,1},{3,2},{4,3},{5,4},{6,5},{7,6},{8,7},{9,8},{10,9},{11,1... | collective-permute-start | bytes 584 | tf_op jit(solution)/shard_map/ppermute | solution.py:40
  132.6 4.7 %collective-permute-start.18 = (f32[2,12,2]{2,1,0:T(8,128)S(1)}, f32[2,12,2]{2,1,0:T(8,128)S(1)}, u32[]{:S(2)}, u32[]{:S(2)}) collective-permute-start(f32[2,12,2]{2,1,0:T(8,128)S(1)} %get-tuple-element.28), channel_id=1, source_target_pairs={{0,1},{1,2},{2,3},{3,4},{4,5},{5,6},{6,7},{7,8},{8,9},{9,10},{10,1... | collective-permute-start | bytes 584 | tf_op jit(solution)/shard_map/ppermute | solution.py:38
  137.1 45.3 %collective-permute-start.3 = (f32[1296,8,1]{0,1,2:T(8,128)S(1)}, f32[1296,8,1]{0,1,2:T(8,128)S(1)}, u32[]{:S(2)}, u32[]{:S(2)}) collective-permute-start(f32[1296,8,1]{0,1,2:T(8,128)S(1)} %copy.63), channel_id=1, source_target_pairs={{1,0},{2,1},{3,2},{4,3},{5,4},{6,5},{7,6},{8,7},{9,8},{10,9},{11,1... | collective-permute-start | bytes 124424 | tf_op jit(solution)/shard_map/ppermute | solution.py:20
  137.6 19.3 %collective-permute-start.20 = (f32[2,2,256]{2,1,0:T(2,128)S(1)}, f32[2,2,256]{2,1,0:T(2,128)S(1)}, u32[]{:S(2)}, u32[]{:S(2)}) collective-permute-start(f32[2,2,256]{2,1,0:T(2,128)S(1)} %get-tuple-element.49), channel_id=1, source_target_pairs={{0,32},{32,64},{64,96},{96,0},{1,33},{33,65},{65,97},{97,1},{2,34}... | collective-permute-start | bytes 12296 | tf_op jit(solution)/shard_map/ppermute | solution.py:38
  137.7 19.3 %collective-permute-start.21 = (f32[2,2,256]{2,1,0:T(2,128)S(1)}, f32[2,2,256]{2,1,0:T(2,128)S(1)}, u32[]{:S(2)}, u32[]{:S(2)}) collective-permute-start(f32[2,2,256]{2,1,0:T(2,128)S(1)} %get-tuple-element.50), channel_id=1, source_target_pairs={{32,0},{64,32},{96,64},{0,96},{33,1},{65,33},{97,65},{1,97},{34,2}... | collective-permute-start | bytes 12296 | tf_op jit(solution)/shard_map/ppermute | solution.py:40
  157.1 6.0 %collective-permute-start.23 = (f32[2,12,2]{2,1,0:T(8,128)S(1)}, f32[2,12,2]{2,1,0:T(8,128)S(1)}, u32[]{:S(2)}, u32[]{:S(2)}) collective-permute-start(f32[2,12,2]{2,1,0:T(8,128)S(1)} %get-tuple-element.25), channel_id=1, source_target_pairs={{1,0},{2,1},{3,2},{4,3},{5,4},{6,5},{7,6},{8,7},{9,8},{10,9},{11,1... | collective-permute-start | bytes 584 | tf_op jit(solution)/shard_map/ppermute | solution.py:40
  162.3 1.2 collective-permute-start.22
  164.4 3.9 %collective-permute-start.24 = (f32[1,256]{1,0:T(1,128)S(1)}, f32[1,256]{1,0:T(1,128)S(1)}, u32[]{:S(2)}, u32[]{:S(2)}) collective-permute-start(f32[1,256]{1,0:T(1,128)S(1)} %get-tuple-element.59), channel_id=1, source_target_pairs={{0,32},{32,64},{64,96},{96,0},{1,33},{33,65},{65,97},{97,1},{2,34}... | collective-permute-start | bytes 3080 | tf_op jit(solution)/shard_map/ppermute | solution.py:38
  164.4 6.8 %collective-permute-start.25 = (f32[1,256]{1,0:T(1,128)S(1)}, f32[1,256]{1,0:T(1,128)S(1)}, u32[]{:S(2)}, u32[]{:S(2)}) collective-permute-start(f32[1,256]{1,0:T(1,128)S(1)} %get-tuple-element.60), channel_id=1, source_target_pairs={{32,0},{64,32},{96,64},{0,96},{33,1},{65,33},{97,65},{1,97},{34,2}... | collective-permute-start | bytes 3080 | tf_op jit(solution)/shard_map/ppermute | solution.py:40
  168.4 14.1 %collective-permute-start = (f32[1296,8,1]{0,1,2:T(8,128)S(1)}, f32[1296,8,1]{0,1,2:T(8,128)S(1)}, u32[]{:S(2)}, u32[]{:S(2)}) collective-permute-start(f32[1296,8,1]{0,1,2:T(8,128)S(1)} %copy.60), channel_id=1, source_target_pairs={{0,1},{1,2},{2,3},{3,4},{4,5},{5,6},{6,7},{7,8},{8,9},{9,10},{10,1... | collective-permute-start | bytes 124424 | tf_op jit(solution)/shard_map/ppermute | solution.py:19
  171.3 4.1 %collective-permute-start.26 = (f32[10,1]{1,0:T(8,128)S(1)}, f32[10,1]{1,0:T(8,128)S(1)}, u32[]{:S(2)}, u32[]{:S(2)}) collective-permute-start(f32[10,1]{1,0:T(8,128)S(1)} %get-tuple-element.47), channel_id=1, source_target_pairs={{0,1},{1,2},{2,3},{3,4},{4,5},{5,6},{6,7},{7,8},{8,9},{9,10},{10,1... | collective-permute-start | bytes 128 | tf_op jit(solution)/shard_map/ppermute | solution.py:38
  175.4 6.9 %collective-permute-start.27 = (f32[10,1]{1,0:T(8,128)S(1)}, f32[10,1]{1,0:T(8,128)S(1)}, u32[]{:S(2)}, u32[]{:S(2)}) collective-permute-start(f32[10,1]{1,0:T(8,128)S(1)} %get-tuple-element.48), channel_id=1, source_target_pairs={{1,0},{2,1},{3,2},{4,3},{5,4},{6,5},{7,6},{8,7},{9,8},{10,9},{11,1... | collective-permute-start | bytes 128 | tf_op jit(solution)/shard_map/ppermute | solution.py:40
where the time goes:
time: 247 us; the launch traced here: 246 us
  local copies, waits for them, and re-layouts  75.3 us (30%)
  other arithmetic  73.7 us (30%)
  starting transfers between devices  56.6 us (23%)
  waiting for transfers between devices  39.2 us (16%)
    unnamed x20, local copies, waits for them, and re-layouts  33.9 us
    ppermute x12, starting transfers between devices, with_halo_2(): lax.ppermute(head, axis, [((i + 1) % count, i) for i in range(count)])  32.2 us
    ppermute x12, waiting for transfers between devices, with_halo_2(): lax.ppermute(tail, axis, [(i, (i + 1) % count) for i in range(count)])  27 us
    mul x1, other arithmetic, body(): ocean * (centre - (flux_east[:, :, 1:] - flux_east[:, :, :-1]) - (flux_no...  20.2 us
    slice x2, local copies, waits for them, and re-layouts, with_halo(): last = lax.slice_in_dim(array, length - width, length, axis=dim)  16.7 us
    mul x1, other arithmetic, body(): analyzed = outer_rim * rim_scale  14.5 us
    unnamed x6, other arithmetic  14.3 us
    scatter x1, local copies, waits for them, and re-layouts, body(): outbox = jnp.zeros((3, devices, slot_cap), jnp.float32).at[:, owners, slo...  11.5 us
  transfers between devices with their start and end apart: 30, of which 12 were waited for; matrix products, arithmetic and copies ran while one was open for 26% of the time, Pallas kernels for 0%

commit v1 on v0

--- a/solution.py
+++ b/solution.py
@@ -6,6 +6,18 @@
 PASSES = 8
 spread_rate = 0.2
 prior_weight = 4.0
+
+
+def link_leaf_up(page):
+    return jnp.concatenate(
+        lax.all_to_all(
+            jnp.stack(jnp.split(page, lax.axis_size("lat"), axis=1)),
+            axis_name="lat",
+            split_axis=0,
+            concat_axis=0,
+        ),
+        axis=1,
+    )
 
 
 def with_halo(array, sides, width):
@@ -77,11 +89,7 @@
         .reshape(3, lat_count, lon_count, slot_cap)
     )
     arrived = lax.all_to_all(
-        lax.all_to_all(outbox, "lat", split_axis=1, concat_axis=1, tiled=True),
-        "lon",
-        split_axis=2,
-        concat_axis=2,
-        tiled=True,
+        link_leaf_up(outbox), "lon", split_axis=2, concat_axis=2, tiled=True
     ).reshape(3, -1)
     totals = blank_grid
     cell_ids = arrived[2].astype(jnp.int32)

time: 247 us -> 247 us (level)
    unnamed x20 -> x24, local copies, waits for them, and re-layouts: 33.9 us -> 34.4 us
    unnamed x6 -> x7, other arithmetic: 14.3 us -> 14.3 us
  transfers between devices with their start and end apart: 30 -> 30, of which waited for: 12 -> 12; matrix products, arithmetic and copies ran while one was open for 26% -> 27% of each run, Pallas kernels for 0% -> 0%
where the time goes in v1:
time: 247 us; the launch traced here: 246 us
  local copies, waits for them, and re-layouts  75.6 us (31%)
  other arithmetic  73.8 us (30%)
  starting transfers between devices  56.6 us (23%)
  waiting for transfers between devices  39.2 us (16%)
    unnamed x24, local copies, waits for them, and re-layouts  34.4 us
    ppermute x12, starting transfers between devices, with_halo_2(): lax.ppermute(head, axis, [((i + 1) % count, i) for i in range(count)])  32.2 us
    ppermute x12, waiting for transfers between devices, with_halo_2(): lax.ppermute(tail, axis, [(i, (i + 1) % count) for i in range(count)])  27 us
    mul x1, other arithmetic, body(): ocean * (centre - (flux_east[:, :, 1:] - flux_east[:, :, :-1]) - (flux_no...  20.3 us
    slice x2, local copies, waits for them, and re-layouts, with_halo(): last = lax.slice_in_dim(array, length - width, length, axis=dim)  16.7 us
    mul x1, other arithmetic, body(): analyzed = outer_rim * rim_scale  14.5 us
    unnamed x7, other arithmetic  14.3 us
    scatter x1, local copies, waits for them, and re-layouts, body(): outbox = jnp.zeros((3, devices, slot_cap), jnp.float32).at[:, owners, slo...  11.5 us
  transfers between devices with their start and end apart: 30, of which 12 were waited for; matrix products, arithmetic and copies ran while one was open for 27% of the time, Pallas kernels for 0%

profile of v1, /device:TPU:1, one launch (start us, length us, event | category | flops | bytes accessed | tf_op | source)
XLA Modules:
  0.0 246.5 jit_solution(8220138398501749848)
XLA Ops:
  0.7 0.8 fusion.119
  1.5 2.5 collective-permute-start.8
  3.9 2.1 collective-permute-start.9
  7.4 0.9 convert_reduce_fusion
  8.3 0.7 or_select_fusion
  9.9 11.5 %scatter_fusion = f32[3,128,8]{0,2,1:T(8,128)S(1)} fusion(f32[3,128,8]{0,2,1:T(8,128)S(1)} %broadcast_in_dim.13, s32[256]{0:T(256)S(1)} %bitcast.45, f32[256,3]{1,0:T(8,128)S(1)} %copy.61), kind=kCustom, calls=%fused_computation.1 | custom fusion | bytes 11264 | tf_op jit(solution)/shard_map/scatter | solution.py:88
  22.7 3.3 %all-to-all-start = ((f32[4,1,768]{2,1,0:T(1,128)}), f32[4,1,768]{2,1,0:T(1,128)S(1)}, u32[]{:S(2)}, u32[]{:S(2)}) async-start(f32[4,1,768]{2,1,0:T(1,128)} %reshape.172), calls=%async_computation | async-start | bytes 24576 | tf_op jit(solution)/shard_map/all_to_all | solution.py:13
  25.9 4.8 %reduce_sum.22 = f32[8,256]{1,0:T(8,128)S(1)} reduce(f32[1296,8,256]{2,1,0:T(8,128)} %param.7, f32[]{:T(128)} %constant.15.clone.1), dimensions={0}, to_apply=%region_2.3 | reduce | flops 2652160 | bytes 10625028 | tf_op jit(solution)/shard_map/reduce_sum | solution.py:76
  30.9 2.2 collective-permute-start.10
  34.4 0.8 copy.66
  35.2 7.7 %all-to-all-start.1 = ((f32[3,4,32,8]{3,1,0,2:T(4,128)}), f32[3,4,32,8]{3,1,0,2:T(4,128)S(1)}, u32[]{:S(2)}, u32[]{:S(2)}) async-start(f32[3,4,32,8]{3,1,0,2:T(4,128)} %copy.66), calls=%async_computation.1 | async-start | bytes 393216 | tf_op jit(solution)/shard_map/all_to_all | solution.py:91
  43.0 8.2 %all-to-all-done.1 = f32[3,4,32,8]{3,1,0,2:T(4,128)S(1)} async-done(((f32[3,4,32,8]{3,1,0,2:T(4,128)}), f32[3,4,32,8]{3,1,0,2:T(4,128)S(1)}, u32[]{:S(2)}, u32[]{:S(2)}) %all-to-all-start.1) | async-done | bytes 12320 | tf_op jit(solution)/shard_map/all_to_all | solution.py:91
  51.9 6.2 %gather_fusion = f32[1024]{0:T(1024)S(1)} fusion(f32[2048]{0:T(1024)S(1)} %bitcast.44, s32[1024]{0:T(1024)S(1)} %broadcast_clamp_fusion), kind=kCustom, calls=%fused_computation | custom fusion | bytes 12288 | tf_op jit(solution)/shard_map/gather | solution.py:97
  58.1 7.0 %scatter_custom_fusion.1 = f32[4096]{0:T(1024)S(1)} fusion(s32[1024]{0:T(1024)S(1)} %get-tuple-element.68, f32[1024]{0:T(1024)S(1)} %subtract_multiply_fusion, f32[]{:T(128)} %constant.15.clone.1), kind=kCustom, calls=%fused_computation.183 | custom fusion | flops 1024 | bytes 16388
  65.1 7.1 %scatter_fusion.1 = f32[4096]{0:T(1024)S(1)} fusion(f32[4096]{0:T(1024)S(1)} %scatter_custom_fusion.1, s32[1024]{0:T(1024)S(1)} %get-tuple-element.67, f32[1024]{0:T(1024)S(1)} %reshape.162), kind=kCustom, calls=%fused_computation.3 | custom fusion | flops 1024 | bytes 16384
  72.2 2.1 collective-permute-start.4
  75.1 0.9 collective-permute-done.4
  76.0 1.0 collective-permute-done.5
  77.0 1.5 collective-permute-start.7
  78.9 1.3 collective-permute-done.7
  80.6 0.8 collective-permute-start.12
  81.4 1.9 collective-permute-start.13
  83.3 9.2 %fusion.102 = (f32[1296,1,256]{2,1,0:T(1,128)S(1)}, f32[1296,1,256]{2,1,0:T(1,128)S(1)}) fusion(f32[1296,8,256]{2,1,0:T(8,128)} %param.7), kind=kLoop, calls=%fused_computation.206 | loop fusion | bytes 5308416 | tf_op jit(solution)/shard_map/slice | solution.py:28
  92.6 1.0 collective-permute-start.2
  93.7 5.8 %collective-permute-start.15 = (f32[2,12,2]{2,1,0:T(8,128)S(1)}, f32[2,12,2]{2,1,0:T(8,128)S(1)}, u32[]{:S(2)}, u32[]{:S(2)}) collective-permute-start(f32[2,12,2]{2,1,0:T(8,128)S(1)} %get-tuple-element.33), channel_id=1, source_target_pairs={{1,0},{2,1},{3,2},{4,3},{5,4},{6,5},{7,6},{8,7},{9,8},{10,9},{11,1... | collective-permute-start | bytes 584 | tf_op jit(solution)/shard_map/ppermute | solution.py:52
  101.6 2.3 collective-permute-start.17
  103.9 7.5 %fusion.103 = (f32[1296,8,1]{2,1,0:T(8,128)}, f32[1296,8,1]{2,1,0:T(8,128)}) fusion(f32[1296,8,256]{2,1,0:T(8,128)} %param.7), kind=kLoop, calls=%fused_computation.207 | loop fusion | bytes 165888 | tf_op jit(solution)/shard_map/slice | solution.py:28
  111.4 20.1 %collective-permute-done.16 = f32[2,2,256]{2,1,0:T(2,128)S(1)} collective-permute-done((f32[2,2,256]{2,1,0:T(2,128)S(1)}, f32[2,2,256]{2,1,0:T(2,128)S(1)}, u32[]{:S(2)}, u32[]{:S(2)}) %collective-permute-start.16) | collective-permute-done | bytes 4128 | tf_op jit(solution)/shard_map/ppermute | solution.py:50
  131.6 1.3 collective-permute-start.19
  133.3 4.1 %copy.75 = f32[1296,8,1]{0,1,2:T(8,128)S(1)} copy(f32[1296,8,1]{2,1,0:T(8,128)} %get-tuple-element.21) | data formatting | bytes 82944
  138.0 2.7 %collective-permute-start.21 = (f32[2,2,256]{2,1,0:T(2,128)S(1)}, f32[2,2,256]{2,1,0:T(2,128)S(1)}, u32[]{:S(2)}, u32[]{:S(2)}) collective-permute-start(f32[2,2,256]{2,1,0:T(2,128)S(1)} %get-tuple-element.54), channel_id=1, source_target_pairs={{32,0},{64,32},{96,64},{0,96},{33,1},{65,33},{97,65},{1,97},{34,2}... | collective-permute-start | bytes 12296 | tf_op jit(solution)/shard_map/ppermute | solution.py:52
  140.8 12.4 %copy.56 = f32[1296,8,256]{0,2,1:T(8,128)} copy(f32[1296,8,256]{2,1,0:T(8,128)} %param.7) | data formatting | bytes 21233664 | tf_op args[0]
  153.2 4.1 %copy.72 = f32[1296,8,1]{0,1,2:T(8,128)S(1)} copy(f32[1296,8,1]{2,1,0:T(8,128)} %get-tuple-element.20) | data formatting | bytes 82944
  157.4 5.2 %collective-permute-start.23 = (f32[2,12,2]{2,1,0:T(8,128)S(1)}, f32[2,12,2]{2,1,0:T(8,128)S(1)}, u32[]{:S(2)}, u32[]{:S(2)}) collective-permute-start(f32[2,12,2]{2,1,0:T(8,128)S(1)} %get-tuple-element.29), channel_id=1, source_target_pairs={{1,0},{2,1},{3,2},{4,3},{5,4},{6,5},{7,6},{8,7},{9,8},{10,9},{11,1... | collective-permute-start | bytes 584 | tf_op jit(solution)/shard_map/ppermute | solution.py:52
  162.7 0.8 collective-permute-done.23
  164.8 2.7 %collective-permute-start.25 = (f32[1,256]{1,0:T(1,128)S(1)}, f32[1,256]{1,0:T(1,128)S(1)}, u32[]{:S(2)}, u32[]{:S(2)}) collective-permute-start(f32[1,256]{1,0:T(1,128)S(1)} %get-tuple-element.64), channel_id=1, source_target_pairs={{32,0},{64,32},{96,64},{0,96},{33,1},{65,33},{97,65},{1,97},{34,2}... | collective-permute-start | bytes 3080 | tf_op jit(solution)/shard_map/ppermute | solution.py:52
  167.5 1.2 collective-permute-done.24
  168.7 2.8 %collective-permute-start = (f32[1296,8,1]{0,1,2:T(8,128)S(1)}, f32[1296,8,1]{0,1,2:T(8,128)S(1)}, u32[]{:S(2)}, u32[]{:S(2)}) collective-permute-start(f32[1296,8,1]{0,1,2:T(8,128)S(1)} %copy.72), channel_id=1, source_target_pairs={{0,1},{1,2},{2,3},{3,4},{4,5},{5,6},{6,7},{7,8},{8,9},{9,10},{10,1... | collective-permute-start | bytes 124424 | tf_op jit(solution)/shard_map/ppermute | solution.py:31
  171.6 4.1 %collective-permute-done.26 = f32[10,1]{1,0:T(8,128)S(1)} collective-permute-done((f32[10,1]{1,0:T(8,128)S(1)}, f32[10,1]{1,0:T(8,128)S(1)}, u32[]{:S(2)}, u32[]{:S(2)}) %collective-permute-start.26) | collective-permute-done | bytes 72 | tf_op jit(solution)/shard_map/ppermute | solution.py:50
  175.7 6.1 %collective-permute-start.27 = (f32[10,1]{1,0:T(8,128)S(1)}, f32[10,1]{1,0:T(8,128)S(1)}, u32[]{:S(2)}, u32[]{:S(2)}) collective-permute-start(f32[10,1]{1,0:T(8,128)S(1)} %get-tuple-element.52), channel_id=1, source_target_pairs={{1,0},{2,1},{3,2},{4,3},{5,4},{6,5},{7,6},{8,7},{9,8},{10,9},{11,1... | collective-permute-start | bytes 128 | tf_op jit(solution)/shard_map/ppermute | solution.py:52
  181.8 0.8 collective-permute-done.27
  182.8 1.8 copy.57
  184.6 1.8 copy.55
  186.4 14.5 %fusion = f32[1296,10,258]{0,2,1:T(8,128)S(1)} fusion(f32[1296,8,1]{0,2,1:T(1,128)S(1)} %copy.82, f32[1296,8,1]{0,2,1:T(1,128)S(1)} %copy.81, f32[1296,1,256]{0,2,1:T(8,128)S(1)} %copy.57, f32[1296,8,256]{0,2,1:T(8,128)} %copy.56, f32[1296,1,256]{0,2,1:T(8,128)S(1)} %copy.55, f32[10,258]{1,0:T(8,128)S(1)} %pad_maximum_fusion.33), kind=kLoop, calls=%fused_computation.5 | loop fusion | flops 30093120 | bytes 26739024 | tf_op jit(solution)/shard_map/mul | solution.py:121
  200.9 5.9 %fusion.6 = f32[1296,8,257]{0,2,1:T(8,128)} fusion(f32[1296,10,258]{0,2,1:T(8,128)S(1)} %fusion, f32[8,257]{1,0:T(8,128)S(1)} %get-tuple-element.38, f32[8,257]{1,0:T(8,128)S(1)} %get-tuple-element.37, f32[1296]{0:T(1024)S(1)} %get-tuple-element.9, f32[1296]{0:T(1024)S(1)} %get-tuple-element.8), kind=kLoop, calls=%fused_computation.17 | loop fusion | flops 13322880 | bytes 32001728 | tf_op jit(solution)/shard_map/mul | solution.py:127
  206.8 7.3 %fusion.3 = f32[1296,9,256]{0,2,1:T(8,128)} fusion(f32[1296,10,258]{0,2,1:T(8,128)S(1)} %fusion, f32[9,256]{1,0:T(8,128)S(1)} %get-tuple-element.40, f32[9,256]{1,0:T(8,128)S(1)} %get-tuple-element.39, f32[1296]{0:T(1024)S(1)} %get-tuple-element.10, f32[1296]{0:T(1024)S(1)} %get-tuple-element.11), kind=kLoop, calls=%fused_computation.12 | loop fusion | flops 14929920 | bytes 35860608 | tf_op jit(solution)/shard_map/mul | solution.py:137
  214.1 20.3 %fusion.8 = f32[1296,8,256]{0,2,1:T(8,128)} fusion(f32[1296,9,256]{0,2,1:T(8,128)} %fusion.3, f32[1296,8,257]{0,2,1:T(8,128)} %fusion.6, f32[1296,10,258]{0,2,1:T(8,128)S(1)} %fusion, f32[8,256]{1,0:T(8,128)S(1)} %convert_element_type.28), kind=kLoop, calls=%fused_computation.21 | loop fusion | flops 13271040 | bytes 63709184 | tf_op jit(solution)/shard_map/mul | solution.py:145
  234.4 12.1 %copy.71 = f32[1296,8,256]{2,1,0:T(8,128)} copy(f32[1296,8,256]{0,2,1:T(8,128)} %fusion.8) | data formatting | bytes 21233664
  (119 shorter events, 12.3 us)
Async XLA Ops:
  0.6 51.0 %copy-start.3 = (s32[2]{0:T(128)S(1)}, s32[2]{0:T(128)}, u32[]{:S(2)}) copy-start(s32[2]{0:T(128)} %constant.55) | copy-start | bytes 28
  0.6 51.1 %copy-start.2 = (s32[2]{0:T(128)S(1)}, s32[2]{0:T(128)}, u32[]{:S(2)}) copy-start(s32[2]{0:T(128)} %constant.52) | copy-start | bytes 28
  0.7 30.1 %copy-start = (s32[8,256]{1,0:T(8,128)S(1)}, s32[8,256]{1,0:T(8,128)}, u32[]{:S(2)}) copy-start(s32[8,256]{1,0:T(8,128)} %param.8) | copy-start | bytes 24580
  1.5 29.3 %collective-permute-start.8 = (s32[2,256]{1,0:T(2,128)S(1)}, s32[2,256]{1,0:T(2,128)S(1)}, u32[]{:S(2)}, u32[]{:S(2)}) collective-permute-start(s32[2,256]{1,0:T(2,128)S(1)} %get-tuple-element.65), channel_id=1, source_target_pairs={{0,32},{32,64},{64,96},{96,0},{1,33},{33,65},{65,97},{97,1},{2,34}... | collective-permute-start | bytes 6152 | tf_op jit(solution)/shard_map/ppermute | solution.py:50
  3.9 26.9 %collective-permute-start.9 = (s32[2,256]{1,0:T(2,128)S(1)}, s32[2,256]{1,0:T(2,128)S(1)}, u32[]{:S(2)}, u32[]{:S(2)}) collective-permute-start(s32[2,256]{1,0:T(2,128)S(1)} %get-tuple-element.66), channel_id=1, source_target_pairs={{32,0},{64,32},{96,64},{0,96},{33,1},{65,33},{97,65},{1,97},{34,2}... | collective-permute-start | bytes 6152 | tf_op jit(solution)/shard_map/ppermute | solution.py:52
  22.7 10.4 %all-to-all-start = ((f32[4,1,768]{2,1,0:T(1,128)}), f32[4,1,768]{2,1,0:T(1,128)S(1)}, u32[]{:S(2)}, u32[]{:S(2)}) async-start(f32[4,1,768]{2,1,0:T(1,128)} %reshape.172), calls=%async_computation | async-start | bytes 24576 | tf_op jit(solution)/shard_map/all_to_all | solution.py:13
  30.9 11.9 %collective-permute-start.10 = (s32[12,2]{1,0:T(8,128)S(1)}, s32[12,2]{1,0:T(8,128)S(1)}, u32[]{:S(2)}, u32[]{:S(2)}) collective-permute-start(s32[12,2]{1,0:T(8,128)S(1)} %get-tuple-element.59), channel_id=1, source_target_pairs={{0,1},{1,2},{2,3},{3,4},{4,5},{5,6},{6,7},{7,8},{8,9},{9,10},{10,1... | collective-permute-start | bytes 296 | tf_op jit(solution)/shard_map/ppermute | solution.py:50
  33.1 9.8 %collective-permute-start.11 = (s32[12,2]{1,0:T(8,128)S(1)}, s32[12,2]{1,0:T(8,128)S(1)}, u32[]{:S(2)}, u32[]{:S(2)}) collective-permute-start(s32[12,2]{1,0:T(8,128)S(1)} %get-tuple-element.60), channel_id=1, source_target_pairs={{1,0},{2,1},{3,2},{4,3},{5,4},{6,5},{7,6},{8,7},{9,8},{10,9},{11,1... | collective-permute-start | bytes 296 | tf_op jit(solution)/shard_map/ppermute | solution.py:52
  35.2 16.0 %all-to-all-start.1 = ((f32[3,4,32,8]{3,1,0,2:T(4,128)}), f32[3,4,32,8]{3,1,0,2:T(4,128)S(1)}, u32[]{:S(2)}, u32[]{:S(2)}) async-start(f32[3,4,32,8]{3,1,0,2:T(4,128)} %copy.66), calls=%async_computation.1 | async-start | bytes 393216 | tf_op jit(solution)/shard_map/all_to_all | solution.py:91
  72.2 3.7 %collective-permute-start.4 = (f32[2,2,256]{2,1,0:T(2,128)S(1)}, f32[2,2,256]{2,1,0:T(2,128)S(1)}, u32[]{:S(2)}, u32[]{:S(2)}) collective-permute-start(f32[2,2,256]{2,1,0:T(2,128)S(1)} %get-tuple-element.61), channel_id=1, source_target_pairs={{0,32},{32,64},{64,96},{96,0},{1,33},{33,65},{65,97},{97,1},{2,34}... | collective-permute-start | bytes 12296 | tf_op jit(solution)/shard_map/ppermute | solution.py:50
  74.3 2.6 %collective-permute-start.5 = (f32[2,2,256]{2,1,0:T(2,128)S(1)}, f32[2,2,256]{2,1,0:T(2,128)S(1)}, u32[]{:S(2)}, u32[]{:S(2)}) collective-permute-start(f32[2,2,256]{2,1,0:T(2,128)S(1)} %get-tuple-element.62), channel_id=1, source_target_pairs={{32,0},{64,32},{96,64},{0,96},{33,1},{65,33},{97,65},{1,97},{34,2}... | collective-permute-start | bytes 12296 | tf_op jit(solution)/shard_map/ppermute | solution.py:52
  77.0 3.2 %collective-permute-start.7 = (f32[2,12,2]{2,1,0:T(8,128)S(1)}, f32[2,12,2]{2,1,0:T(8,128)S(1)}, u32[]{:S(2)}, u32[]{:S(2)}) collective-permute-start(f32[2,12,2]{2,1,0:T(8,128)S(1)} %get-tuple-element.35), channel_id=1, source_target_pairs={{1,0},{2,1},{3,2},{4,3},{5,4},{6,5},{7,6},{8,7},{9,8},{10,9},{11,1... | collective-permute-start | bytes 584 | tf_op jit(solution)/shard_map/ppermute | solution.py:52
  78.5 1.7 collective-permute-start.6
  80.6 13.1 %collective-permute-start.12 = (f32[2,2,256]{2,1,0:T(2,128)S(1)}, f32[2,2,256]{2,1,0:T(2,128)S(1)}, u32[]{:S(2)}, u32[]{:S(2)}) collective-permute-start(f32[2,2,256]{2,1,0:T(2,128)S(1)} %get-tuple-element.57), channel_id=1, source_target_pairs={{0,32},{32,64},{64,96},{96,0},{1,33},{33,65},{65,97},{97,1},{2,34}... | collective-permute-start | bytes 12296 | tf_op jit(solution)/shard_map/ppermute | solution.py:50
  81.4 12.2 %collective-permute-start.13 = (f32[2,2,256]{2,1,0:T(2,128)S(1)}, f32[2,2,256]{2,1,0:T(2,128)S(1)}, u32[]{:S(2)}, u32[]{:S(2)}) collective-permute-start(f32[2,2,256]{2,1,0:T(2,128)S(1)} %get-tuple-element.58), channel_id=1, source_target_pairs={{32,0},{64,32},{96,64},{0,96},{33,1},{65,33},{97,65},{1,97},{34,2}... | collective-permute-start | bytes 12296 | tf_op jit(solution)/shard_map/ppermute | solution.py:52
  92.6 90.2 %collective-permute-start.2 = (f32[1296,1,256]{2,0,1:T(8,128)S(1)}, f32[1296,1,256]{2,0,1:T(8,128)}, u32[]{:S(2)}, u32[]{:S(2)}) collective-permute-start(f32[1296,1,256]{2,0,1:T(8,128)S(1)} %copy.74), channel_id=1, source_target_pairs={{32,0},{64,32},{96,64},{0,96},{33,1},{65,33},{97,65},{1,97},{34,2}... | collective-permute-start | bytes 3981320 | tf_op jit(solution)/shard_map/ppermute | solution.py:32
  93.7 6.7 %collective-permute-start.15 = (f32[2,12,2]{2,1,0:T(8,128)S(1)}, f32[2,12,2]{2,1,0:T(8,128)S(1)}, u32[]{:S(2)}, u32[]{:S(2)}) collective-permute-start(f32[2,12,2]{2,1,0:T(8,128)S(1)} %get-tuple-element.33), channel_id=1, source_target_pairs={{1,0},{2,1},{3,2},{4,3},{5,4},{6,5},{7,6},{8,7},{9,8},{10,9},{11,1... | collective-permute-start | bytes 584 | tf_op jit(solution)/shard_map/ppermute | solution.py:52
  99.6 1.2 collective-permute-start.14
  99.7 85.0 %collective-permute-start.1 = (f32[1296,1,256]{2,0,1:T(8,128)S(1)}, f32[1296,1,256]{2,0,1:T(8,128)}, u32[]{:S(2)}, u32[]{:S(2)}) collective-permute-start(f32[1296,1,256]{2,0,1:T(8,128)S(1)} %copy.73), channel_id=1, source_target_pairs={{0,32},{32,64},{64,96},{96,0},{1,33},{33,65},{65,97},{97,1},{2,34}... | collective-permute-start | bytes 3981320 | tf_op jit(solution)/shard_map/ppermute | solution.py:31
  101.1 30.4 %collective-permute-start.16 = (f32[2,2,256]{2,1,0:T(2,128)S(1)}, f32[2,2,256]{2,1,0:T(2,128)S(1)}, u32[]{:S(2)}, u32[]{:S(2)}) collective-permute-start(f32[2,2,256]{2,1,0:T(2,128)S(1)} %get-tuple-element.55), channel_id=1, source_target_pairs={{0,32},{32,64},{64,96},{96,0},{1,33},{33,65},{65,97},{97,1},{2,34}... | collective-permute-start | bytes 12296 | tf_op jit(solution)/shard_map/ppermute | solution.py:50
  101.6 39.2 %copy-start.1 = (f32[2,1296]{1,0:T(2,128)S(1)}, f32[2,1296]{1,0:T(2,128)}, u32[]{:S(2)}) copy-start(f32[2,1296]{1,0:T(2,128)} %param.9) | copy-start | bytes 31108
  101.6 29.9 %collective-permute-start.17 = (f32[2,2,256]{2,1,0:T(2,128)S(1)}, f32[2,2,256]{2,1,0:T(2,128)S(1)}, u32[]{:S(2)}, u32[]{:S(2)}) collective-permute-start(f32[2,2,256]{2,1,0:T(2,128)S(1)} %get-tuple-element.56), channel_id=1, source_target_pairs={{32,0},{64,32},{96,64},{0,96},{33,1},{65,33},{97,65},{1,97},{34,2}... | collective-permute-start | bytes 12296 | tf_op jit(solution)/shard_map/ppermute | solution.py:52
  131.6 6.0 %collective-permute-start.19 = (f32[2,12,2]{2,1,0:T(8,128)S(1)}, f32[2,12,2]{2,1,0:T(8,128)S(1)}, u32[]{:S(2)}, u32[]{:S(2)}) collective-permute-start(f32[2,12,2]{2,1,0:T(8,128)S(1)} %get-tuple-element.31), channel_id=1, source_target_pairs={{1,0},{2,1},{3,2},{4,3},{5,4},{6,5},{7,6},{8,7},{9,8},{10,9},{11,1... | collective-permute-start | bytes 584 | tf_op jit(solution)/shard_map/ppermute | solution.py:52
  132.9 4.7 %collective-permute-start.18 = (f32[2,12,2]{2,1,0:T(8,128)S(1)}, f32[2,12,2]{2,1,0:T(8,128)S(1)}, u32[]{:S(2)}, u32[]{:S(2)}) collective-permute-start(f32[2,12,2]{2,1,0:T(8,128)S(1)} %get-tuple-element.32), channel_id=1, source_target_pairs={{0,1},{1,2},{2,3},{3,4},{4,5},{5,6},{6,7},{7,8},{8,9},{9,10},{10,1... | collective-permute-start | bytes 584 | tf_op jit(solution)/shard_map/ppermute | solution.py:50
  137.4 45.3 %collective-permute-start.3 = (f32[1296,8,1]{0,1,2:T(8,128)S(1)}, f32[1296,8,1]{0,1,2:T(8,128)S(1)}, u32[]{:S(2)}, u32[]{:S(2)}) collective-permute-start(f32[1296,8,1]{0,1,2:T(8,128)S(1)} %copy.75), channel_id=1, source_target_pairs={{1,0},{2,1},{3,2},{4,3},{5,4},{6,5},{7,6},{8,7},{9,8},{10,9},{11,1... | collective-permute-start | bytes 124424 | tf_op jit(solution)/shard_map/ppermute | solution.py:32
  138.0 19.3 %collective-permute-start.20 = (f32[2,2,256]{2,1,0:T(2,128)S(1)}, f32[2,2,256]{2,1,0:T(2,128)S(1)}, u32[]{:S(2)}, u32[]{:S(2)}) collective-permute-start(f32[2,2,256]{2,1,0:T(2,128)S(1)} %get-tuple-element.53), channel_id=1, source_target_pairs={{0,32},{32,64},{64,96},{96,0},{1,33},{33,65},{65,97},{97,1},{2,34}... | collective-permute-start | bytes 12296 | tf_op jit(solution)/shard_map/ppermute | solution.py:50
  138.0 19.2 %collective-permute-start.21 = (f32[2,2,256]{2,1,0:T(2,128)S(1)}, f32[2,2,256]{2,1,0:T(2,128)S(1)}, u32[]{:S(2)}, u32[]{:S(2)}) collective-permute-start(f32[2,2,256]{2,1,0:T(2,128)S(1)} %get-tuple-element.54), channel_id=1, source_target_pairs={{32,0},{64,32},{96,64},{0,96},{33,1},{65,33},{97,65},{1,97},{34,2}... | collective-permute-start | bytes 12296 | tf_op jit(solution)/shard_map/ppermute | solution.py:52
  157.4 6.0 %collective-permute-start.23 = (f32[2,12,2]{2,1,0:T(8,128)S(1)}, f32[2,12,2]{2,1,0:T(8,128)S(1)}, u32[]{:S(2)}, u32[]{:S(2)}) collective-permute-start(f32[2,12,2]{2,1,0:T(8,128)S(1)} %get-tuple-element.29), channel_id=1, source_target_pairs={{1,0},{2,1},{3,2},{4,3},{5,4},{6,5},{7,6},{8,7},{9,8},{10,9},{11,1... | collective-permute-start | bytes 584 | tf_op jit(solution)/shard_map/ppermute | solution.py:52
  162.6 1.2 collective-permute-start.22
  164.7 3.9 %collective-permute-start.24 = (f32[1,256]{1,0:T(1,128)S(1)}, f32[1,256]{1,0:T(1,128)S(1)}, u32[]{:S(2)}, u32[]{:S(2)}) collective-permute-start(f32[1,256]{1,0:T(1,128)S(1)} %get-tuple-element.63), channel_id=1, source_target_pairs={{0,32},{32,64},{64,96},{96,0},{1,33},{33,65},{65,97},{97,1},{2,34}... | collective-permute-start | bytes 3080 | tf_op jit(solution)/shard_map/ppermute | solution.py:50
  164.8 6.8 %collective-permute-start.25 = (f32[1,256]{1,0:T(1,128)S(1)}, f32[1,256]{1,0:T(1,128)S(1)}, u32[]{:S(2)}, u32[]{:S(2)}) collective-permute-start(f32[1,256]{1,0:T(1,128)S(1)} %get-tuple-element.64), channel_id=1, source_target_pairs={{32,0},{64,32},{96,64},{0,96},{33,1},{65,33},{97,65},{1,97},{34,2}... | collective-permute-start | bytes 3080 | tf_op jit(solution)/shard_map/ppermute | solution.py:52
  168.7 14.1 %collective-permute-start = (f32[1296,8,1]{0,1,2:T(8,128)S(1)}, f32[1296,8,1]{0,1,2:T(8,128)S(1)}, u32[]{:S(2)}, u32[]{:S(2)}) collective-permute-start(f32[1296,8,1]{0,1,2:T(8,128)S(1)} %copy.72), channel_id=1, source_target_pairs={{0,1},{1,2},{2,3},{3,4},{4,5},{5,6},{6,7},{7,8},{8,9},{9,10},{10,1... | collective-permute-start | bytes 124424 | tf_op jit(solution)/shard_map/ppermute | solution.py:31
  171.6 4.1 %collective-permute-start.26 = (f32[10,1]{1,0:T(8,128)S(1)}, f32[10,1]{1,0:T(8,128)S(1)}, u32[]{:S(2)}, u32[]{:S(2)}) collective-permute-start(f32[10,1]{1,0:T(8,128)S(1)} %get-tuple-element.51), channel_id=1, source_target_pairs={{0,1},{1,2},{2,3},{3,4},{4,5},{5,6},{6,7},{7,8},{8,9},{9,10},{10,1... | collective-permute-start | bytes 128 | tf_op jit(solution)/shard_map/ppermute | solution.py:50
  175.7 6.9 %collective-permute-start.27 = (f32[10,1]{1,0:T(8,128)S(1)}, f32[10,1]{1,0:T(8,128)S(1)}, u32[]{:S(2)}, u32[]{:S(2)}) collective-permute-start(f32[10,1]{1,0:T(8,128)S(1)} %get-tuple-element.52), channel_id=1, source_target_pairs={{1,0},{2,1},{3,2},{4,3},{5,4},{6,5},{7,6},{8,7},{9,8},{10,9},{11,1... | collective-permute-start | bytes 128 | tf_op jit(solution)/shard_map/ppermute | solution.py:52
